TPU v7x, 32 devices: a whole 2x2x4 slice. The times are simulated.
32 devices in a mesh: ops: 8 (over z, core), blk: 4 (over y, x).
Axes of the slice: x: 2, y: 2, z: 4, core: 2. Of those that a mesh axis runs over, the one named last changes fastest.
Arguments:
- psi: bfloat16 [2048, 1024], P('blk'), may hold values from -6 to 6
- left_blocks: bfloat16 [64, 16, 128, 128], P('ops', 'blk'), may hold values from -0.5 to 0.5
- right_ops: bfloat16 [64, 1024, 1024], P(('ops', 'blk')), may hold values from -0.046875 to 0.046875
- block_target: int32 [64, 16], P('ops'), may hold values from 0 to 15
- left_partner: int32 [64], P('ops'), may hold values from 0 to 63, as said below
- block_len: int32 [16], replicated, may hold values from 1 to 128, 1536 in all
Outputs:
- sigma: bfloat16 [2048, 1024], P('blk', 'ops')
Inputs may be any that keep to these rules, and one draw needn't show every extreme that they name: left_partner is a permutation of 0 to 63 that maps each aligned group of 8 operators onto itself.
All inputs are finite; a program needn't handle non-finite values.
Results may differ from a plain program's by a relative error of at most 0.018.
Values may be sent and summed in bfloat16 or wider, within the bound.
A program may use at most 128 MiB of HBM per device.

v0:
```python
import jax
import jax.numpy as jnp
from jax import lax
from jax.sharding import PartitionSpec as P


def add_blocks(running, mixed, targets):
    for source in range(mixed.shape[0]):
        where = targets[source]
        current = lax.dynamic_index_in_dim(running, where, 0, keepdims=False)
        running = lax.dynamic_update_index_in_dim(running, current + mixed[source], where, 0)
    return running


def local(psi, left_blocks, right_ops, block_target, left_partner, block_len):
    group_size = left_blocks.shape[0]
    local_blocks = left_blocks.shape[1]
    block_rows = left_blocks.shape[2]
    columns = psi.shape[1]
    blocks_all = block_target.shape[1]
    column_index = lax.axis_index("blk")
    group_index = lax.axis_index("ops")
    first_op = group_index * group_size
    row_index = jnp.arange(block_rows, dtype=jnp.int32)
    live_rows = row_index[None, :] < block_len[:, None]
    live_local = lax.dynamic_slice_in_dim(live_rows, column_index * local_blocks, local_blocks, 0)
    states = psi.reshape(local_blocks, block_rows, columns) * live_local[:, :, None].astype(
        jnp.bfloat16
    )
    blank = jnp.zeros((blocks_all, block_rows, columns), jnp.float32)
    all_states, all_blocks = (
        lax.all_gather(states, "blk", axis=0, tiled=True),
        lax.all_gather(left_blocks, "blk", axis=1, tiled=True),
    )
    stacked = all_states.reshape(blocks_all * block_rows, columns)
    local_ops = right_ops.shape[0]

    def apply_own(step, running):
        image = jnp.dot(stacked, right_ops[step], preferred_element_type=jnp.float32).astype(
            jnp.bfloat16
        )
        image = image.reshape(blocks_all, block_rows, columns)
        owner = left_partner[column_index * local_ops + step] - first_op
        mixed = jnp.einsum(
            "qab,qbr->qar", all_blocks[owner], image, preferred_element_type=jnp.float32
        )
        return add_blocks(running, mixed, block_target[owner])

    partial_sum = lax.fori_loop(0, local_ops, apply_own, blank)
    flat_sum = partial_sum.reshape(blocks_all * block_rows, columns)
    owned = lax.psum_scatter(
        flat_sum.astype(jnp.bfloat16), "blk", scatter_dimension=0, tiled=True
    ).astype(jnp.float32)
    owned = lax.psum_scatter(
        owned.astype(jnp.bfloat16), "ops", scatter_dimension=1, tiled=True
    ).astype(jnp.float32)
    result = owned.reshape(local_blocks, block_rows, -1) * live_local[:, :, None].astype(
        jnp.float32
    )
    return result.reshape(local_blocks * block_rows, -1).astype(jnp.bfloat16)


def solution(mesh):
    return jax.shard_map(
        local,
        mesh=mesh,
        in_specs=(
            P("blk", None),
            P("ops", "blk", None, None),
            P(("ops", "blk"), None, None),
            P("ops", None),
            P("ops"),
            P(),
        ),
        out_specs=P("blk", "ops"),
        check_vma=False,
    )
```

profile of v0, /device:TPU:0, one launch (start us, length us, event | category | flops | bytes accessed | tf_op | source)
XLA Modules:
  0.0 390.6 jit_solution(13257646383401635814)
XLA Ops:
  8.1 2.3 broadcast_multiply_fusion
  10.5 54.0 %all-gather.3.cloned.1.call-done = bf16[8,16,128,128]{3,2,1,0:T(8,128)(2,1)} async-done(((bf16[8,4,128,128]{3,2,1,0:T(8,128)(2,1)}), bf16[8,16,128,128]{3,2,1,0:T(8,128)(2,1)}) %all-gather.3.cloned.1.call-update) | async-done | bytes 4194320 | tf_op jit(solution)/shard_map/all_gather | solution.py:33
  64.5 54.4 %all-gather.5.cloned.1.call-done = bf16[16,128,1024]{2,1,0:T(8,128)(2,1)} async-done(((bf16[4,128,1024]{2,1,0:T(8,128)(2,1)}), bf16[16,128,1024]{2,1,0:T(8,128)(2,1)}) %all-gather.5.cloned.1.call-update) | async-done | bytes 4194320 | tf_op jit(solution)/shard_map/all_gather | solution.py:32
  119.0 4.3 %broadcast_in_dim.56 = f32[16,128,1024]{2,1,0:T(8,128)} broadcast(f32[]{:T(128)} %constant.126.clone.1), dimensions={} | broadcast | bytes 8388612 | tf_op jit(solution)/shard_map/broadcast_in_dim | solution.py:30
  123.2 165.1 %while.15 = (s32[]{:T(128)}, f32[16,128,1024]{2,1,0:T(8,128)}, s32[]{:T(128)}, s32[8]{0:T(128)S(1)}, s32[]{:T(128)}, /*index=5*/s32[8,16]{1,0:T(8,128)}, bf16[8,...) while((s32[]{:T(128)}, f32[16,128,1024]{2,1,0:T(8,128)}, ...), condition=%wide.region_1.2_spmd, body=%wide.region_0.1_spmd.sunk | while | flops 4836032512 | bytes 57148476 | solution.py:49
  155.5 9.3 %convert_bitcast_fusion.2 = bf16[2048,1024]{0,1:T(8,128)(2,1)} fusion(bf16[2048,1024]{1,0:T(8,128)(2,1)} %get-tuple-element.375, bf16[2,1024,1024]{2,1,0:T(8,128)(2,1)} %get-tuple-element.374, s32[]{:T(128)S(6)} %copy.32), kind=kOutput, calls=%fused_computation.clone.1 | convolution fusion | flops 4297064448 | bytes 10485764 | tf_op jit(solution)/shard_map/while/body/eval_jaxpr/dot_general | solution.py:39
  164.9 6.4 %copy.13 = bf16[2048,1024]{1,0:T(8,128)(2,1)} copy(bf16[2048,1024]{0,1:T(8,128)(2,1)} %convert_bitcast_fusion.2) | data formatting | bytes 8388608 | tf_op jit(solution)/shard_map/while/body/eval_jaxpr/reshape | solution.py:42
  171.3 3.6 fusion.56
  174.9 2.0 fusion.57
  178.8 2.0 fusion.59
  194.3 2.0 fusion.67
  200.1 2.0 fusion.70
  202.0 1.9 fusion.71
  238.2 9.3 %convert_bitcast_fusion.2 = bf16[2048,1024]{0,1:T(8,128)(2,1)} fusion(bf16[2048,1024]{1,0:T(8,128)(2,1)} %get-tuple-element.375, bf16[2,1024,1024]{2,1,0:T(8,128)(2,1)} %get-tuple-element.374, s32[]{:T(128)S(6)} %copy.32), kind=kOutput, calls=%fused_computation.clone.1 | convolution fusion | flops 4297064448 | bytes 10485764 | tf_op jit(solution)/shard_map/while/body/eval_jaxpr/dot_general | solution.py:39
  247.5 6.4 %copy.13 = bf16[2048,1024]{1,0:T(8,128)(2,1)} copy(bf16[2048,1024]{0,1:T(8,128)(2,1)} %convert_bitcast_fusion.2) | data formatting | bytes 8388608 | tf_op jit(solution)/shard_map/while/body/eval_jaxpr/reshape | solution.py:42
  254.0 3.6 fusion.56
  257.6 2.0 fusion.57
  276.8 2.0 fusion.67
  278.7 2.0 fusion.68
  282.6 2.0 fusion.70
  288.4 6.0 %convert_element_type.33 = bf16[16,128,1024]{2,1,0:T(8,128)(2,1)} convert(f32[16,128,1024]{2,1,0:T(8,128)} %get-tuple-element.217) | non-fusion elementwise | flops 2097152 | bytes 12582912 | tf_op jit(solution)/shard_map/convert_element_type | solution.py:52
  294.5 52.6 %reduce-scatter.5.cloned.1.call-done = bf16[512,1024]{1,0:T(8,128)(2,1)} async-done(((bf16[2048,1024]{1,0:T(8,128)(2,1)}), bf16[512,1024]{1,0:T(8,128)(2,1)}) %reduce-scatter.5.cloned.1.call-update) | async-done | bytes 1048592 | tf_op jit(solution)/shard_map/reduce_scatter | solution.py:51
  347.1 2.3 copy.10
  349.4 32.8 %reduce-scatter.7.cloned.1.call-done = bf16[128,512]{1,0:T(8,128)(2,1)} async-done(((bf16[1024,512]{1,0:T(8,128)(2,1)}), bf16[128,512]{1,0:T(8,128)(2,1)}) %reduce-scatter.7.cloned.1.call-update) | async-done | bytes 131088
  (43 shorter events, 51.7 us)
Async XLA Ops:
  6.5 116.7 %copy-start = (s32[8]{0:T(128)S(1)}, s32[8]{0:T(128)}, u32[]{:S(2)}) copy-start(s32[8]{0:T(128)} %param.12) | copy-start | bytes 100
  6.5 58.0 %all-gather.3.cloned.1.call-start = ((), (), s32[]{:S(2)}) async-start(), calls=%async_computation.2 | async-start | bytes 5242880 | tf_op jit(solution)/shard_map/all_gather | solution.py:33
  7.3 111.7 %all-gather.5.cloned.1.call-start = ((), (), s32[]{:S(2)}) async-start(), calls=%async_computation.3 | async-start | bytes 5242880 | tf_op jit(solution)/shard_map/all_gather | solution.py:32
  10.5 336.6 %reduce-scatter.5.cloned.1.call-start = ((), (), s32[]{:S(2)}) async-start(), calls=%async_computation.4 | async-start | bytes 5242880 | tf_op jit(solution)/shard_map/reduce_scatter | solution.py:51
  294.4 87.8 %reduce-scatter.7.cloned.1.call-start = ((), (), s32[]{:S(2)}) async-start(), calls=%async_computation.5 | async-start | bytes 1179648
Sparse Core Ops, SparseCore 0:
  9.2 55.2 all-gather.2
  66.4 52.5 all-gather.4
  294.6 52.5 reduce-scatter.4
  349.5 32.6 reduce-scatter.6
where the time goes:
time: 394 us; the launch traced here: 391 us
  waiting for transfers between devices  195 us (49%)
  other arithmetic  71 us (18%)
  loops' own time  60.5 us (15%)
  matrix products  25.8 us (7%)
  local copies, waits for them, and re-layouts  25.3 us (6%)
  between operations  13.1 us (3%)
    dynamic_update_slice x32, other arithmetic, add_blocks(): lax.dynamic_update_index_in_dim(running, current + mixed[source], where, 0)  61.8 us
    another operation x1, loops' own time, local(): partial_sum = lax.fori_loop(0, local_ops, apply_own, blank)  60.5 us
    all_gather x1, waiting for transfers between devices, local(): lax.all_gather(states, 'blk', axis=0, tiled=True)  54.4 us
    all_gather x1, waiting for transfers between devices, local(): lax.all_gather(left_blocks, 'blk', axis=1, tiled=True)  54 us
    reduce_scatter x1, waiting for transfers between devices, local(): lax.psum_scatter(flat_sum.astype(jnp.bfloat16), 'blk', scatter_dimension=...  52.6 us
    unnamed x5, waiting for transfers between devices  33.6 us
    dot_general x2, matrix products, apply_own(): jnp.dot(stacked, right_ops[step], preferred_element_type=jnp.float32)  18.7 us
    reshape x2, local copies, waits for them, and re-layouts, apply_own(): image = image.reshape(blocks_all, block_rows, columns)  12.9 us
  transfers between devices with their start and end apart: 4, of which 4 were waited for; matrix products, arithmetic and copies ran while one was open for 1% of the time, Pallas kernels for 0%

commit v1 on v0

v1 whole, which is shorter than its diff:
```python
import functools

import jax
import jax.numpy as jnp
from jax import lax
from jax.experimental import pallas as pl
from jax.experimental.pallas import tpu as pltpu
from jax.sharding import PartitionSpec as P

MESH = pl.DeviceIdType.MESH
VMEM = pltpu.VMEM
DMA = pltpu.SemaphoreType.DMA


def across(c, d, n):
    out, bit = 0, 1
    while bit < n:
        have = (c // bit) % 2
        out = out + bit * (1 - have if d & bit else have)
        bit *= 2
    return out


def remote(src, dst, send, recv, to):
    return pltpu.make_async_remote_copy(
        src_ref=src, dst_ref=dst, send_sem=send, recv_sem=recv, device_id=to, device_id_type=MESH
    )


def greet(targets):
    barrier = pltpu.get_barrier_semaphore()
    for to in targets:
        pl.semaphore_signal(barrier, inc=1, device_id=to, device_id_type=MESH)
    pl.semaphore_wait(barrier, len(targets))


def places(n_ops, n_blk):
    g, c = lax.axis_index("ops"), lax.axis_index("blk")
    chips = n_ops // 2
    z, core = g // 2, g % 2
    peers = [across(c, d, n_blk) for d in range(n_blk)]
    up = [((z + e) % chips) * 2 + core for e in range(chips)]
    down = [((z + chips - e) % chips) * 2 + core for e in range(chips)]
    partner = z * 2 + (1 - core)
    return g, c, z, core, peers, up, down, partner


def gather_kernel(
    n_ops, n_blk, psi_ref, left_ref, pair_ref, psi_out, left_out, stage,
    send_a, recv_a, send_l, recv_l, send_b, recv_b, send_p, recv_p,
):
    g, c, z, core, peers, up, down, partner = places(n_ops, n_blk)
    chips = n_ops // 2
    piece = psi_ref.shape[0] // n_ops
    group = left_ref.shape[0]
    local_ops = group // n_blk
    rows = pl.ds(pl.multiple_of(g * piece, piece), piece)

    greet(
        [(g, peers[d]) for d in range(1, n_blk)]
        + [(up[e], c) for e in range(1, chips)]
        + [(partner, c)]
    )
    first = [
        remote(psi_ref.at[rows], psi_out.at[c, rows], send_a.at[d], recv_a.at[d], (g, peers[d]))
        for d in range(n_blk)
    ]
    order = list(range(n_blk - 1, 0, -1))
    for d in order:
        first[d].start()
    for j in range(group):
        stage[j] = left_ref[pair_ref[j]]
    lefts = [
        remote(
            stage.at[pl.ds(peers[d] * local_ops, local_ops)],
            left_out.at[c], send_l.at[d], recv_l.at[d], (g, peers[d]),
        )
        for d in range(n_blk)
    ]
    for d in order:
        lefts[d].start()
    psi_out[c] = psi_ref[...]
    left_out[c] = stage[pl.ds(c * local_ops, local_ops)]

    sent = []
    for d in order:
        first[d].wait_recv()
        here = psi_out.at[peers[d], rows]
        for e in range(1, chips):
            copy = remote(here, here, send_b.at[d, e], recv_b.at[d, e], (up[e], c))
            copy.start()
            sent.append(copy)
        copy = remote(here, here, send_p.at[d, 0], recv_p.at[d, 0], (partner, c))
        copy.start()
        sent.append(copy)
    for d in order:
        for e in range(1, chips):
            at = pl.ds(pl.multiple_of(down[e] * piece, piece), piece)
            here = psi_out.at[peers[d], at]
            remote(here, here, send_b.at[d, e], recv_b.at[d, e], (up[e], c)).wait_recv()
            copy = remote(here, here, send_p.at[d, e], recv_p.at[d, e], (partner, c))
            copy.start()
            sent.append(copy)
    for d in order:
        for e in range(chips):
            other = down[e] - core + (1 - core)
            at = pl.ds(pl.multiple_of(other * piece, piece), piece)
            here = psi_out.at[peers[d], at]
            remote(here, here, send_p.at[d, e], recv_p.at[d, e], (partner, c)).wait_recv()
        lefts[d].wait_recv()
    for copy in sent:
        copy.wait_send()
    for d in order:
        first[d].wait_send()
        lefts[d].wait_send()


def mix_kernel(target_ref, len_ref, psi_ref, left_ref, out_ref, total):
    blocks, block_rows, columns = psi_ref.shape
    local_ops = total.shape[0]
    per = left_ref.shape[2]
    total[...] = jnp.zeros_like(total)
    lane = lax.broadcasted_iota(jnp.int32, (1, block_rows), 1)

    def one(q, carry):
        left = left_ref[q // per, :, q % per].reshape(local_ops * block_rows, block_rows)
        left = jnp.where(lane < len_ref[q], left, jnp.zeros_like(left))
        for half in range(columns // 512):
            cols = pl.ds(half * 512, 512)
            mixed = jnp.dot(left, psi_ref[q, :, cols], preferred_element_type=jnp.float32)
            for r in range(local_ops):
                t = target_ref[r, q]
                total[r, t, :, cols] += mixed[r * block_rows : (r + 1) * block_rows]
        return carry

    lax.fori_loop(0, blocks, one, 0)

    def out(t, carry):
        for r in range(local_ops):
            out_ref[r, t] = total[r, t].astype(out_ref.dtype)
        return carry

    lax.fori_loop(0, blocks, out, 0)


def reduce_kernel(
    n_ops, n_blk, y_hbm, r_hbm, out_ref,
    y_v, r_v, part, recv1, send2, recv2, send3, recv3,
    y_sem, r_sem, send_1, recv_1, send_2, recv_2, send_3, recv_3,
):
    g, c, z, core, peers, up, down, partner = places(n_ops, n_blk)
    chips = n_ops // 2
    local_ops = r_v.shape[0]
    rows = y_v.shape[2]
    wide = 2 * out_ref.shape[1]
    thin = out_ref.shape[1]
    order = list(range(n_blk - 1, -1, -1))

    def load(d):
        at = pl.ds(pl.multiple_of(peers[d] * rows, rows), rows)
        return pltpu.make_async_copy(y_hbm.at[:, at], y_v.at[d], y_sem.at[d])

    weights = pltpu.make_async_copy(r_hbm, r_v, r_sem)
    load(order[0]).start()
    weights.start()
    for d in order[1:]:
        load(d).start()
    greet(
        [(g, peers[d]) for d in range(1, n_blk)]
        + [(up[e], c) for e in range(1, chips)]
        + [(partner, c)]
    )
    weights.wait()

    def compute(d):
        load(d).wait()

        def tile(j, carry):
            cols = pl.ds(pl.multiple_of(j * wide, wide), wide)
            acc = jnp.dot(y_v[d, 0], r_v[0, :, cols], preferred_element_type=jnp.float32)
            for r in range(1, local_ops):
                acc += jnp.dot(y_v[d, r], r_v[r, :, cols], preferred_element_type=jnp.float32)
            acc = acc.astype(jnp.bfloat16)
            part[d, 0, j] = acc[:, :thin]
            part[d, 1, j] = acc[:, thin:]
            return carry

        lax.fori_loop(0, chips, tile, 0)

    swaps = [
        remote(part.at[d, 1 - core], recv1.at[d], send_1.at[d], recv_1.at[d], (partner, c))
        for d in range(n_blk)
    ]
    outs = [
        remote(send2.at[d], recv2.at[d], send_2.at[d], recv_2.at[d], (g, peers[d]))
        for d in range(n_blk)
    ]

    def join(d):
        swaps[d].wait_recv()

        def add(j, carry):
            send2[d, j] = (
                part[d, core, j].astype(jnp.float32) + recv1[d, j].astype(jnp.float32)
            ).astype(jnp.bfloat16)
            return carry

        lax.fori_loop(0, chips, add, 0)
        if d:
            outs[d].start()

    before = None
    for d in order:
        compute(d)
        swaps[d].start()
        if before is not None:
            join(before)
        before = d
    join(before)
    for d in order[:-1]:
        outs[d].wait_recv()

    def gathered(j):
        acc = send2[0, j].astype(jnp.float32)
        for d in range(1, n_blk):
            acc += recv2[d, j].astype(jnp.float32)
        return acc

    lasts = [
        remote(send3.at[e], recv3.at[e], send_3.at[e], recv_3.at[e], (up[e], c))
        for e in range(chips)
    ]
    for e in range(1, chips):
        send3[e] = gathered((z + e) % chips).astype(jnp.bfloat16)
        lasts[e].start()
    acc = gathered(z)
    for e in range(1, chips):
        lasts[e].wait_recv()
        acc += recv3[e].astype(jnp.float32)
    out_ref[...] = acc.astype(out_ref.dtype)
    for d in range(n_blk):
        swaps[d].wait_send()
        if d:
            outs[d].wait_send()
    for e in range(1, chips):
        lasts[e].wait_send()


def local(n_ops, n_blk, psi, left_blocks, right_ops, block_target, left_partner, block_len):
    group, local_blocks, block_rows, _ = left_blocks.shape
    my_rows, columns = psi.shape
    local_ops = right_ops.shape[0]
    blocks = block_target.shape[1]
    chips = n_ops // 2
    thin = columns // n_ops
    bf16 = jnp.bfloat16
    in_vmem = pl.BlockSpec(memory_space=pltpu.VMEM)
    in_smem = pl.BlockSpec(memory_space=pltpu.SMEM)
    in_hbm = pl.BlockSpec(memory_space=pl.ANY)

    pair = left_partner - lax.axis_index("ops") * group
    psi_all, left_all = pl.pallas_call(
        functools.partial(gather_kernel, n_ops, n_blk),
        out_shape=(
            jax.ShapeDtypeStruct((n_blk, my_rows, columns), bf16),
            jax.ShapeDtypeStruct((n_blk, local_ops, local_blocks, block_rows, block_rows), bf16),
        ),
        in_specs=[in_vmem, in_vmem, in_smem],
        out_specs=(in_vmem, in_vmem),
        scratch_shapes=[
            VMEM(left_blocks.shape, bf16),
            DMA((n_blk,)), DMA((n_blk,)), DMA((n_blk,)), DMA((n_blk,)),
            DMA((n_blk, chips)), DMA((n_blk, chips)), DMA((n_blk, chips)), DMA((n_blk, chips)),
        ],
        compiler_params=pltpu.CompilerParams(collective_id=0, has_side_effects=True),
        name="gather",
    )(psi, left_blocks, pair)

    c = lax.axis_index("blk")
    mine = lax.dynamic_slice_in_dim(pair, c * local_ops, local_ops, 0)
    targets = block_target[mine]
    mixed = pl.pallas_call(
        mix_kernel,
        out_shape=jax.ShapeDtypeStruct((local_ops, blocks, block_rows, columns), bf16),
        in_specs=[in_smem, in_smem, in_vmem, in_vmem],
        out_specs=in_vmem,
        scratch_shapes=[VMEM((local_ops, blocks, block_rows, columns), jnp.float32)],
        compiler_params=pltpu.CompilerParams(vmem_limit_bytes=63 * 2**20),
        name="mix",
    )(targets, block_len, psi_all.reshape(blocks, block_rows, columns), left_all)

    sums = pl.pallas_call(
        functools.partial(reduce_kernel, n_ops, n_blk),
        out_shape=jax.ShapeDtypeStruct((my_rows, thin), bf16),
        in_specs=[in_hbm, in_hbm],
        out_specs=in_vmem,
        scratch_shapes=[
            VMEM((n_blk, local_ops, my_rows, columns), bf16),
            VMEM(right_ops.shape, bf16),
            VMEM((n_blk, 2, chips, my_rows, thin), bf16),
            VMEM((n_blk, chips, my_rows, thin), bf16),
            VMEM((n_blk, chips, my_rows, thin), bf16),
            VMEM((n_blk, chips, my_rows, thin), bf16),
            VMEM((chips, my_rows, thin), bf16),
            VMEM((chips, my_rows, thin), bf16),
            DMA((n_blk,)), DMA, DMA((n_blk,)), DMA((n_blk,)), DMA((n_blk,)), DMA((n_blk,)),
            DMA((chips,)), DMA((chips,)),
        ],
        compiler_params=pltpu.CompilerParams(
            collective_id=1, has_side_effects=True, vmem_limit_bytes=63 * 2**20
        ),
        name="reduce",
    )(mixed.reshape(local_ops, blocks * block_rows, columns), right_ops)

    lens = lax.dynamic_slice_in_dim(block_len, c * local_blocks, local_blocks, 0)
    live = jnp.arange(block_rows, dtype=jnp.int32)[None, :] < lens[:, None]
    shaped = sums.reshape(local_blocks, block_rows, thin)
    return jnp.where(live[:, :, None], shaped, jnp.zeros_like(shaped)).reshape(my_rows, thin)


def solution(mesh):
    return jax.shard_map(
        functools.partial(local, mesh.shape["ops"], mesh.shape["blk"]),
        mesh=mesh,
        in_specs=(
            P("blk", None),
            P("ops", "blk", None, None),
            P(("ops", "blk"), None, None),
            P("ops", None),
            P("ops"),
            P(),
        ),
        out_specs=P("blk", "ops"),
        check_vma=False,
    )
```

time: 394 us -> 114 us (0.29)
  waiting for transfers between devices: 195 us -> 0 us
  Pallas kernels: 0 us -> 109 us
  other arithmetic: 71 us -> 2.51 us
  loops' own time: 60.5 us -> 0 us
  matrix products: 25.8 us -> 0 us
  local copies, waits for them, and re-layouts: 25.3 us -> 1.86 us
  between operations: 13.1 us -> 0.02 us
    pallas_call x0 -> x3, Pallas kernels: none -> 109 us  [the longest x1 49 us: local(): pl.pallas_call(functools.partial(gather_kernel, n_ops, n_blk), out_shape=...]
    all_gather x2 -> x0, waiting for transfers between devices: 108 us -> none  [the longest x1 54.4 us: local(): lax.all_gather(states, 'blk', axis=0, tiled=True)]
    dynamic_update_slice x32 -> x0, other arithmetic: 61.8 us -> none  [add_blocks(): lax.dynamic_update_index_in_dim(running, current + mixed[source], where, 0)]
    another operation x1 -> x0, loops' own time: 60.5 us -> none  [local(): partial_sum = lax.fori_loop(0, local_ops, apply_own, blank)]
    reduce_scatter x1 -> x0, waiting for transfers between devices: 52.6 us -> none  [local(): lax.psum_scatter(flat_sum.astype(jnp.bfloat16), 'blk', scatter_dimension=...]
    unnamed x5 -> x0, waiting for transfers between devices: 33.6 us -> none
    dot_general x4 -> x0, matrix products: 25.8 us -> none  [the longest x2 18.7 us: apply_own(): jnp.dot(stacked, right_ops[step], preferred_element_type=jnp.float32)]
    reshape x2 -> x0, local copies, waits for them, and re-layouts: 12.9 us -> none  [apply_own(): image = image.reshape(blocks_all, block_rows, columns)]
  transfers between devices with their start and end apart: 4 -> 0, of which waited for: 4 -> 0; matrix products, arithmetic and copies ran while one was open for 1% -> 0% of each run, Pallas kernels for 0% -> 0%
where the time goes in v1:
time: 114 us; the launch traced here: 113 us
  Pallas kernels  109 us (96%)
  other arithmetic  2.51 us (2%)
  local copies, waits for them, and re-layouts  1.86 us (2%)
    pallas_call x1, Pallas kernels, local(): pl.pallas_call(functools.partial(gather_kernel, n_ops, n_blk), out_shape=...  49 us
    pallas_call x1, Pallas kernels, local(): pl.pallas_call(functools.partial(reduce_kernel, n_ops, n_blk), out_shape=...  47.5 us
    pallas_call x1, Pallas kernels, local(): pl.pallas_call(mix_kernel, out_shape=jax.ShapeDtypeStruct((local_ops, blo...  12.3 us

profile of v1, /device:TPU:0, one launch (start us, length us, event | category | flops | bytes accessed | tf_op | source)
XLA Modules:
  0.0 113.1 jit_solution(13689541681254802418)
XLA Ops:
  0.0 0.0 copy-start
  0.0 0.7 dynamic_slice.6
  0.7 0.1 fusion
  0.8 0.7 broadcast_subtract_fusion.pair_ref
  1.5 0.0 copy-start.1
  1.5 0.1 compare_select_fusion
  1.6 0.0 copy-done
  1.6 1.1 gather_fusion
  2.7 0.0 copy-done.1
  2.7 49.0 %gather.7 = (bf16[4,512,1024]{2,1,0:T(8,128)(2,1)}, bf16[4,2,4,128,128]{4,3,2,1,0:T(8,128)(2,1)}) custom-call(bf16[512,1024]{1,0:T(8,128)(2,1)} %psi_ref.1, bf16[8,4,128,128]{3,2,1,0:T(8,128)(2,1)} %left_ref.1, s32[8]{0:T(128)} %copy-done.1), custom_call_target="tpu_custom_call" | custom-call | tf_op jit(solution)/shard_map/gather/pallas_call | solution.py:262
  51.6 12.3 %mix.1 = bf16[2,16,128,1024]{3,2,1,0:T(8,128)(2,1)} custom-call(s32[2,16]{1,0:T(2,128)} %gather_fusion, s32[16]{0:T(128)} %len_ref.1, bf16[16,128,1024]{2,1,0:T(8,128)(2,1)} %bitcast.5, bf16[4,2,4,128,128]{4,3,2,1,0:T(8,128)(2,1)} %get-tuple-element.8.left_ref), custom_call_target="tpu_custom_call" | custom-call | tf_op jit(solution)/shard_map/mix/pallas_call | solution.py:282
  63.9 47.5 %reduce.1 = bf16[512,128]{1,0:T(8,128)(2,1)} custom-call(bf16[2,2048,1024]{2,1,0:T(8,128)(2,1)} %bitcast.4, bf16[2,1024,1024]{2,1,0:T(8,128)(2,1)} %r_hbm.1), custom_call_target="tpu_custom_call" | custom-call | tf_op jit(solution)/shard_map/reduce/pallas_call | solution.py:292
  111.4 1.7 %broadcast_select_fusion = bf16[512,128]{1,0:T(8,128)(2,1)} fusion(bf16[512,128]{1,0:T(8,128)(2,1)} %reduce.1, pred[512]{0:T(512)(128)(4,1)S(1)} %fusion), kind=kLoop, calls=%fused_computation.1 | loop fusion | flops 65536 | bytes 262656 | tf_op jit(solution)/shard_map/jit(_where)/select_n | solution.py:318
  (1 shorter events, 0.0 us)
Async XLA Ops:
  0.0 1.6 %copy-start = (s32[8,16]{1,0:T(8,128)S(1)}, s32[8,16]{1,0:T(8,128)}, u32[]{:S(2)}) copy-start(s32[8,16]{1,0:T(8,128)} %param.9) | copy-start | bytes 1540
  1.5 1.2 %copy-start.1 = (s32[8]{0:T(128)}, s32[8]{0:T(128)S(1)}, u32[]{:S(2)}) copy-start(s32[8]{0:T(128)S(1)} %broadcast_subtract_fusion.pair_ref) | copy-start | bytes 100

commit v2 on v1

v2 whole, which is shorter than its diff:
```python
import functools

import jax
import jax.numpy as jnp
from jax import lax
from jax.experimental import pallas as pl
from jax.experimental.pallas import tpu as pltpu
from jax.sharding import PartitionSpec as P

MESH = pl.DeviceIdType.MESH
VMEM = pltpu.VMEM
DMA = pltpu.SemaphoreType.DMA


def across(c, d, n):
    out, bit = 0, 1
    while bit < n:
        have = (c // bit) % 2
        out = out + bit * (1 - have if d & bit else have)
        bit *= 2
    return out


def remote(src, dst, send, recv, to):
    return pltpu.make_async_remote_copy(
        src_ref=src, dst_ref=dst, send_sem=send, recv_sem=recv, device_id=to, device_id_type=MESH
    )


def greet(targets):
    barrier = pltpu.get_barrier_semaphore()
    for to in targets:
        pl.semaphore_signal(barrier, inc=1, device_id=to, device_id_type=MESH)
    pl.semaphore_wait(barrier, len(targets))


def places(n_ops, n_blk):
    g, c = lax.axis_index("ops"), lax.axis_index("blk")
    chips = n_ops // 2
    z, core = g // 2, g % 2
    peers = [across(c, d, n_blk) for d in range(n_blk)]
    up = [((z + e) % chips) * 2 + core for e in range(chips)]
    down = [((z + chips - e) % chips) * 2 + core for e in range(chips)]
    partner = z * 2 + (1 - core)
    return g, c, z, core, peers, up, down, partner


def shares(my_rows, n_ops):
    piece = max(my_rows * 3 // 4 // n_ops // 16, 1) * 16
    return piece, (my_rows - piece * n_ops) // 2


def gather_kernel(
    n_ops, n_blk, psi_ref, left_ref, pair_ref, psi_out, left_out, stage,
    send_a, recv_a, send_l, recv_l, send_c, recv_c, send_z, recv_z, send_p, recv_p,
):
    g, c, z, core, peers, up, down, partner = places(n_ops, n_blk)
    chips = n_ops // 2
    piece, straight = shares(psi_ref.shape[0], n_ops)
    group = left_ref.shape[0]
    local_ops = group // n_blk

    def rows_of(chip, which):
        return pl.ds(pl.multiple_of((chip * 2 + which) * piece, piece), piece)

    def straight_of(which):
        return pl.ds(pl.multiple_of(piece * n_ops + which * straight, 16), straight)

    greet(
        [(g, peers[d]) for d in range(1, n_blk)]
        + [(up[1], c), (down[1], c), (partner, c)]
    )
    order = list(range(1, n_blk))
    mine = rows_of(z, core)
    first = {
        d: remote(psi_ref.at[mine], psi_out.at[c, mine], send_a.at[d], recv_a.at[d], (g, peers[d]))
        for d in order
    }
    for d in order:
        first[d].start()
    for j in range(group):
        stage[j] = left_ref[lax.rem(pair_ref[j], group)]
    lefts = {
        d: remote(
            stage.at[pl.ds(peers[d] * local_ops, local_ops)],
            left_out.at[c], send_l.at[d], recv_l.at[d], (g, peers[d]),
        )
        for d in order
    }
    at = straight_of(core) if straight else None
    plain = {
        d: remote(psi_ref.at[at], psi_out.at[c, at], send_c.at[d], recv_c.at[d], (g, peers[d]))
        for d in order if straight
    }
    for d in order:
        if straight:
            plain[d].start()
    for d in order:
        lefts[d].start()
    psi_out[c] = psi_ref[...]
    left_out[c] = stage[pl.ds(c * local_ops, local_ops)]

    def hop(d, h, way, source):
        here = psi_out.at[peers[d], rows_of(source, core)]
        to = (g + 2, c) if way == 0 else (g - 2, c)
        return remote(here, here, send_z.at[way, d, h], recv_z.at[way, d, h], to)

    def share(d, h, way, source, which):
        here = psi_out.at[peers[d], rows_of(source, which)]
        return remote(here, here, send_p.at[way, d, h], recv_p.at[way, d, h], (partner, c))

    def can_send(h, way):
        if way == 0:
            return jnp.logical_and(z >= h, z < chips - 1)
        return jnp.logical_and(z < chips - h, z > 0)

    def has(h, way):
        return z >= h if way == 0 else z < chips - h

    def source_of(h, way):
        return z - h if way == 0 else z + h

    for h in range(chips):
        for d in order:
            if h == 0:
                first[d].wait_recv()
                share(d, 0, 0, z, core).start()
            for way in range(2):
                source = source_of(h, way)
                if h:
                    @pl.when(has(h, way))
                    def _(d=d, h=h, way=way, source=source):
                        hop(d, h - 1, way, source).wait_recv()
                        share(d, h, way, source, core).start()
                if h < chips - 1:
                    @pl.when(can_send(h, way))
                    def _(d=d, h=h, way=way, source=source):
                        hop(d, h, way, source).start()
    for d in order if straight else []:
        plain[d].wait_recv()
        here = psi_out.at[peers[d], at]
        remote(here, here, send_c.at[d + n_blk], recv_c.at[d + n_blk], (partner, c)).start()
    for d in order:
        if straight:
            here = psi_out.at[peers[d], straight_of(1 - core)]
            remote(here, here, send_c.at[d + n_blk], recv_c.at[d + n_blk], (partner, c)).wait()
            plain[d].wait_send()
        lefts[d].wait()
        first[d].wait_send()
        share(d, 0, 0, z, 1 - core).wait()
        for way in range(2):
            for h in range(chips):
                source = source_of(h, way)
                if h:
                    @pl.when(has(h, way))
                    def _(d=d, h=h, way=way, source=source):
                        share(d, h, way, source, 1 - core).wait()
                if h < chips - 1:
                    @pl.when(can_send(h, way))
                    def _(d=d, h=h, way=way, source=source):
                        hop(d, h, way, source).wait_send()


def mix_kernel(target_ref, pair_ref, len_ref, psi_ref, left_ref, out_ref, total):
    blocks, block_rows, columns = psi_ref.shape
    local_ops = total.shape[0]
    per = left_ref.shape[2]
    group = target_ref.shape[0]
    c = lax.axis_index("blk")
    total[...] = jnp.zeros_like(total)
    lane = lax.broadcasted_iota(jnp.int32, (1, block_rows), 1)
    row = lax.broadcasted_iota(jnp.int32, (block_rows, 1), 0)
    owners = [lax.rem(pair_ref[c * local_ops + r], group) for r in range(local_ops)]

    def one(q, carry):
        left = left_ref[q // per, :, q % per].reshape(local_ops * block_rows, block_rows)
        left = jnp.where(lane < len_ref[q], left, jnp.zeros_like(left))
        mixed = jnp.dot(left, psi_ref[q], preferred_element_type=jnp.float32)
        for r in range(local_ops):
            total[r, target_ref[owners[r], q]] += mixed[r * block_rows : (r + 1) * block_rows]
        return carry

    lax.fori_loop(0, blocks, one, 0, unroll=4)

    def out(t, carry):
        for r in range(local_ops):
            kept = total[r, t]
            kept = jnp.where(row < len_ref[t], kept, jnp.zeros_like(kept))
            out_ref[r, t] = kept.astype(out_ref.dtype)
        return carry

    lax.fori_loop(0, blocks, out, 0)


def reduce_kernel(
    n_ops, n_blk, y_hbm, r_hbm, out_ref,
    y_v, r_v, part, recv1, send2, recv2, send3, recv3,
    y_sem, r_sem, send_1, recv_1, send_2, recv_2, send_3, recv_3,
):
    g, c, z, core, peers, up, down, partner = places(n_ops, n_blk)
    chips = n_ops // 2
    local_ops = r_hbm.shape[0]
    rows = y_v.shape[2]
    thin = out_ref.shape[1]
    wide = 2 * thin
    order = list(range(n_blk - 1, -1, -1))

    def load(d):
        at = pl.ds(pl.multiple_of(peers[d] * rows, rows), rows)
        return pltpu.make_async_copy(y_hbm.at[:, at], y_v.at[d], y_sem.at[d])

    def weights(k):
        j = (z + 1 + k) % chips
        cols = pl.ds(pl.multiple_of(j * wide, wide), wide)
        return pltpu.make_async_copy(r_hbm.at[:, :, cols], r_v.at[k], r_sem.at[k])

    weights(0).start()
    for d in order:
        load(d).start()
    for k in range(1, chips):
        weights(k).start()
    greet(
        [(g, peers[d]) for d in range(1, n_blk)]
        + [(up[e], c) for e in range(1, chips)]
        + [(partner, c)]
    )

    def product(k, d):
        acc = jnp.dot(y_v[d, 0], r_v[k, 0], preferred_element_type=jnp.float32)
        for r in range(1, local_ops):
            acc += jnp.dot(y_v[d, r], r_v[k, r], preferred_element_type=jnp.float32)
        acc = acc.astype(jnp.bfloat16)
        part[k, 0, d] = acc[:, :thin]
        part[k, 1, d] = acc[:, thin:]

    def swap(k):
        return remote(
            part.at[k, 1 - core], recv1.at[k], send_1.at[k], recv_1.at[k], (partner, c)
        )

    def spread(k, d):
        return remote(
            send2.at[k, d], recv2.at[k, d], send_2.at[k, d], recv_2.at[k, d], (g, peers[d])
        )

    def last(k):
        return remote(
            send3.at[k], recv3.at[k], send_3.at[k], recv_3.at[k], (up[k + 1], c)
        )

    def compute(k):
        weights(k).wait()
        if k == 0:
            for d in order:
                load(d).wait()
                product(k, d)
        else:
            lax.fori_loop(0, n_blk, lambda d, carry: (product(k, d), carry)[1], 0)
        swap(k).start()

    def join(k):
        swap(k).wait_recv()
        for d in order:
            send2[k, d] = (
                part[k, core, d].astype(jnp.float32) + recv1[k, d].astype(jnp.float32)
            ).astype(jnp.bfloat16)
            if d:
                spread(k, d).start()

    def finish(k):
        acc = send2[k, 0].astype(jnp.float32)
        for d in range(1, n_blk):
            spread(k, d).wait_recv()
            acc += recv2[k, d].astype(jnp.float32)
        if k < chips - 1:
            send3[k] = acc.astype(jnp.bfloat16)
            last(k).start()
            return
        for e in range(chips - 1):
            last(e).wait_recv()
            acc += recv3[e].astype(jnp.float32)
        out_ref[...] = acc.astype(out_ref.dtype)

    compute(0)
    for k in range(1, chips):
        compute(k)
        join(k - 1)
        if k > 2:
            finish(k - 3)
    join(chips - 1)
    for k in range(max(chips - 3, 0), chips):
        finish(k)
    for k in range(chips):
        swap(k).wait_send()
        for d in range(1, n_blk):
            spread(k, d).wait_send()
        if k < chips - 1:
            last(k).wait_send()


def local(n_ops, n_blk, psi, left_blocks, right_ops, block_target, left_partner, block_len):
    group, local_blocks, block_rows, _ = left_blocks.shape
    my_rows, columns = psi.shape
    local_ops = right_ops.shape[0]
    blocks = block_target.shape[1]
    chips = n_ops // 2
    thin = columns // n_ops
    bf16 = jnp.bfloat16
    in_vmem = pl.BlockSpec(memory_space=pltpu.VMEM)
    in_smem = pl.BlockSpec(memory_space=pltpu.SMEM)
    in_hbm = pl.BlockSpec(memory_space=pl.ANY)

    psi_all, left_all = pl.pallas_call(
        functools.partial(gather_kernel, n_ops, n_blk),
        out_shape=(
            jax.ShapeDtypeStruct((n_blk, my_rows, columns), bf16),
            jax.ShapeDtypeStruct((n_blk, local_ops, local_blocks, block_rows, block_rows), bf16),
        ),
        in_specs=[in_vmem, in_vmem, in_smem],
        out_specs=(in_vmem, in_vmem),
        scratch_shapes=[
            VMEM(left_blocks.shape, bf16),
            DMA((n_blk,)), DMA((n_blk,)), DMA((n_blk,)), DMA((n_blk,)),
            DMA((2 * n_blk,)), DMA((2 * n_blk,)),
            DMA((2, n_blk, chips)), DMA((2, n_blk, chips)),
            DMA((2, n_blk, chips)), DMA((2, n_blk, chips)),
        ],
        compiler_params=pltpu.CompilerParams(collective_id=0, has_side_effects=True),
        name="gather",
    )(psi, left_blocks, left_partner)

    step = min(columns, 256)
    mixed = pl.pallas_call(
        mix_kernel,
        grid=(columns // step,),
        out_shape=jax.ShapeDtypeStruct((local_ops, blocks, block_rows, columns), bf16),
        in_specs=[
            in_smem, in_smem, in_smem,
            pl.BlockSpec((blocks, block_rows, step), lambda i: (0, 0, i)),
            pl.BlockSpec(left_all.shape, lambda i: (0,) * 5),
        ],
        out_specs=pl.BlockSpec((local_ops, blocks, block_rows, step), lambda i: (0, 0, 0, i)),
        scratch_shapes=[VMEM((local_ops, blocks, block_rows, step), jnp.float32)],
        compiler_params=pltpu.CompilerParams(vmem_limit_bytes=63 * 2**20),
        name="mix",
    )(
        block_target, left_partner, block_len,
        psi_all.reshape(blocks, block_rows, columns), left_all,
    )

    return pl.pallas_call(
        functools.partial(reduce_kernel, n_ops, n_blk),
        out_shape=jax.ShapeDtypeStruct((my_rows, thin), bf16),
        in_specs=[in_hbm, in_hbm],
        out_specs=in_vmem,
        scratch_shapes=[
            VMEM((n_blk, local_ops, my_rows, columns), bf16),
            VMEM((chips, local_ops, columns, 2 * thin), bf16),
            VMEM((chips, 2, n_blk, my_rows, thin), bf16),
            VMEM((chips, n_blk, my_rows, thin), bf16),
            VMEM((chips, n_blk, my_rows, thin), bf16),
            VMEM((chips, n_blk, my_rows, thin), bf16),
            VMEM((chips, my_rows, thin), bf16),
            VMEM((chips, my_rows, thin), bf16),
            DMA((n_blk,)), DMA((chips,)), DMA((chips,)), DMA((chips,)),
            DMA((chips, n_blk)), DMA((chips, n_blk)), DMA((chips,)), DMA((chips,)),
        ],
        compiler_params=pltpu.CompilerParams(
            collective_id=1, has_side_effects=True, vmem_limit_bytes=63 * 2**20
        ),
        name="reduce",
    )(mixed.reshape(local_ops, blocks * block_rows, columns), right_ops)


def solution(mesh):
    return jax.shard_map(
        functools.partial(local, mesh.shape["ops"], mesh.shape["blk"]),
        mesh=mesh,
        in_specs=(
            P("blk", None),
            P("ops", "blk", None, None),
            P(("ops", "blk"), None, None),
            P("ops", None),
            P("ops"),
            P(),
        ),
        out_specs=P("blk", "ops"),
        check_vma=False,
    )
```

time: 114 us -> 83.7 us (0.73)
  Pallas kernels: 109 us -> 81.9 us
  other arithmetic: 2.51 us -> 0 us
    pallas_call x1, Pallas kernels: 49 us -> 35 us  [local(): pl.pallas_call(functools.partial(gather_kernel, n_ops, n_blk), out_shape=...]
    pallas_call x1, Pallas kernels: 47.5 us -> 36 us  [local(): pl.pallas_call(functools.partial(reduce_kernel, n_ops, n_blk), out_shape=...]
    select_n x2 -> x0, other arithmetic: 1.77 us -> none  [the longest x1 1.7 us: local(): jnp.where(live[:, :, None], shaped, jnp.zeros_like(shaped))]
    unnamed x4 -> x1, local copies, waits for them, and re-layouts: 0.01 us -> 1.57 us
    pallas_call x1, Pallas kernels: 12.3 us -> 10.8 us  [local(): pl.pallas_call(mix_kernel, grid=(columns // step,), out_shape=jax.ShapeDt...]
where the time goes in v2:
time: 83.7 us; the launch traced here: 83.4 us
  Pallas kernels  81.9 us (98%)
  local copies, waits for them, and re-layouts  1.57 us (2%)
    pallas_call x1, Pallas kernels, local(): pl.pallas_call(functools.partial(reduce_kernel, n_ops, n_blk), out_shape=...  36 us
    pallas_call x1, Pallas kernels, local(): pl.pallas_call(functools.partial(gather_kernel, n_ops, n_blk), out_shape=...  35 us
    pallas_call x1, Pallas kernels, local(): pl.pallas_call(mix_kernel, grid=(columns // step,), out_shape=jax.ShapeDt...  10.8 us

profile of v2, /device:TPU:0, one launch (start us, length us, event | category | flops | bytes accessed | tf_op | source)
XLA Modules:
  0.0 83.4 jit_solution(4637055168566520700)
XLA Ops:
  0.0 35.0 %gather.1 = (bf16[4,512,1024]{2,1,0:T(8,128)(2,1)}, bf16[4,2,4,128,128]{4,3,2,1,0:T(8,128)(2,1)}) custom-call(bf16[512,1024]{1,0:T(8,128)(2,1)} %psi_ref.1, bf16[8,4,128,128]{3,2,1,0:T(8,128)(2,1)} %left_ref.1, s32[8]{0:T(128)} %pair_ref.3), custom_call_target="tpu_custom_call" | custom-call | tf_op jit(solution)/shard_map/gather/pallas_call | solution.py:313
  35.0 10.8 %mix.1 = bf16[2,16,128,1024]{3,2,1,0:T(8,128)(2,1)} custom-call(s32[8,16]{1,0:T(8,128)} %target_ref.1, s32[8]{0:T(128)} %pair_ref.3, s32[16]{0:T(128)} %len_ref.1, bf16[16,128,1024]{2,1,0:T(8,128)(2,1)} %bitcast.3, bf16[4,2,4,128,128]{4,3,2,1,0:T(8,128)(2,1)} %get-tuple-element.8.left_ref), custom_call_target="tpu_custom_call" | custom-call | tf_op jit(solution)/shard_map/mix/pallas_call | solution.py:333
  45.8 36.0 %reduce.1 = bf16[512,128]{1,0:T(8,128)(2,1)} custom-call(bf16[2,2048,1024]{2,1,0:T(8,128)(2,1)} %bitcast.2, bf16[2,1024,1024]{2,1,0:T(8,128)(2,1)} %r_hbm.1), custom_call_target="tpu_custom_call" | custom-call | tf_op jit(solution)/shard_map/reduce/pallas_call | solution.py:351
  81.9 1.6 %copy.8 = bf16[512,128]{1,0:T(8,128)(2,1)} copy(bf16[512,128]{1,0:T(8,128)(2,1)} %reduce.1) | data formatting | bytes 262144
